TPU v7x, 128 devices: a whole 4x4x4 slice. The times are simulated.
128 devices in a mesh: lat: 32 (over y, z, core), fld: 4 (over x).
Axes of the slice: x: 4, y: 4, z: 4, core: 2. Of those that a mesh axis runs over, the one named last changes fastest.
Arguments:
- grid_fields: bfloat16 [96, 1280, 2560], P('fld', 'lat'), may hold values from -6 to 6
- assign: int32 [320], replicated, may hold values from 0 to 319, each once
- limits: int32 [3], replicated, may hold values from 60 to 319, as said below
- legendre: bfloat16 [320, 641, 640], P('lat', None, 'fld'), may hold values from -0.25 to 0.25
- synth_one: bfloat16 [320, 320, 320], P('lat'), may hold values from -0.3125 to 0.3125
- synth_two: bfloat16 [320, 160, 160], P('lat'), may hold values from -0.5 to 0.5
- synth_three: bfloat16 [320, 80, 80], P('lat'), may hold values from -0.625 to 0.625
Outputs:
- spectrum: bfloat16 [96, 2, 320, 641], P('fld', None, 'lat')
- grid_one: float32 [96, 640, 1280], P('fld', 'lat')
- grid_two: float32 [96, 320, 640], P('fld', 'lat')
- grid_three: float32 [96, 160, 320], P('fld', 'lat')
Inputs may be any that keep to these rules, and one draw needn't show every extreme that they name: assign is a permutation; slot q stands for the wavenumbers assign[q] and 639 - assign[q]. limits[0] is 319, limits[2] is 60, and limits[1] lies between 120 and 159.
All inputs are finite; a program needn't handle non-finite values.
Results may differ from a plain program's by a relative error of at most 0.0077.
Values may be sent and summed in bfloat16 or wider, within the bound.
A program may use at most 128 MiB of HBM per device.

v0:
```python
import math

import jax
import jax.numpy as jnp
from jax import lax
from jax.experimental import pallas as pl
from jax.experimental.pallas import tpu as pltpu
from jax.sharding import PartitionSpec as P

MESH = pl.DeviceIdType.MESH
F32 = jnp.float32
BF16 = jnp.bfloat16
NLAT = 32
NFLD = 4
FLD = 24
ROWS = 40
LON = 2560
PAIR = 10
SENT = (20, 10, 5)
LEVELS = (320, 160, 80)
NT = (((1,), (1,)), ((), ()))


def sincos(turns):
    quarter = jnp.floor(turns * 4.0 + 0.5)
    y = (turns * 4.0 - quarter) * (math.pi / 2)
    y2 = y * y
    s = y * (1.0 + y2 * (-1.0 / 6 + y2 * (1.0 / 120 - y2 * (1.0 / 5040))))
    c = 1.0 + y2 * (-0.5 + y2 * (1.0 / 24 + y2 * (-1.0 / 720 + y2 * (1.0 / 40320))))
    k = quarter - 4.0 * jnp.floor(quarter * 0.25)
    odd = (k == 1.0) | (k == 3.0)
    sin_v = jnp.where(odd, c, s)
    cos_v = jnp.where(odd, s, c)
    sin_v = jnp.where(k >= 2.0, -sin_v, sin_v)
    cos_v = jnp.where((k == 1.0) | (k == 2.0), -cos_v, cos_v)
    return cos_v, sin_v


def turns_of(product, period):
    return (product - period * jnp.floor(product * (1.0 / period))) * (1.0 / period)


def fill_table(cols_ref, first, count, period, scale, tiles, store):
    wave = jnp.broadcast_to(cols_ref[pl.ds(first, count), 0:1], (count, 128))
    amp = jnp.broadcast_to(cols_ref[pl.ds(first, count), 1:2], (count, 128)) * scale
    comp = jnp.broadcast_to(cols_ref[pl.ds(first, count), 2:3], (count, 128))
    lane = lax.broadcasted_iota(jnp.int32, (count, 128), 1).astype(F32)
    cos_v, sin_v = sincos(turns_of(wave * lane + comp * (period // 4), float(period)))
    cos_d, sin_d = sincos(turns_of(wave * 128.0, float(period)))
    cos_v, sin_v = cos_v * amp, sin_v * amp
    for a in range(tiles):
        store(a, cos_v)
        if a + 1 < tiles:
            cos_v, sin_v = cos_v * cos_d - sin_v * sin_d, sin_v * cos_d + cos_v * sin_d


def lat_peer(k):
    return lax.rem(lax.axis_index("lat") + k, NLAT)


def greet():
    barrier = pltpu.get_barrier_semaphore()
    fld = lax.axis_index("fld")
    lat = lax.axis_index("lat")

    def one(k, carry):
        pl.semaphore_signal(barrier, inc=1, device_id=(lat_peer(k), fld), device_id_type=MESH)
        return carry

    lax.fori_loop(1, NLAT, one, 0)
    for k in range(1, NFLD):
        pl.semaphore_signal(
            barrier, inc=1, device_id=(lat, lax.rem(fld + k, NFLD)), device_id_type=MESH
        )
    pl.semaphore_wait(barrier, NLAT + NFLD - 2)


def to_lat(src, dst, send_sem, recv_sem, k):
    return pltpu.make_async_remote_copy(
        src_ref=src,
        dst_ref=dst,
        send_sem=send_sem,
        recv_sem=recv_sem,
        device_id=(lat_peer(k), lax.axis_index("fld")),
        device_id_type=MESH,
    )


def to_fld(part, send_sem, recv_sem, k):
    fld = lax.rem(lax.axis_index("fld") + k, NFLD)
    return pltpu.make_async_remote_copy(
        src_ref=part,
        dst_ref=part,
        send_sem=send_sem,
        recv_sem=recv_sem,
        device_id=(lax.axis_index("lat"), fld),
        device_id_type=MESH,
    )


def each(first, count, act):
    def one(k, carry):
        act(k)
        return carry

    lax.fori_loop(first, count, one, 0)


def pack_pair(q, raw, main, extra, own):
    a = raw[q].astype(F32)
    t = [a[:, 128 * k : 128 * k + 128] for k in range(5)]
    last = a[:, 640:641]
    lane = lax.broadcasted_iota(jnp.int32, (a.shape[0], 128), 1)
    r = [None, None] + [pltpu.roll(t[k], 63, 1) for k in (2, 3, 4)]
    main[q, own, 0:128] = t[0].astype(BF16)
    main[q, own, 128:256] = t[1].astype(BF16)
    main[q, own, 256:384] = jnp.where(lane < 63, r[2], r[3]).astype(BF16)
    main[q, own, 384:512] = jnp.where(lane < 63, r[3], r[4]).astype(BF16)
    tail = jnp.where(lane < 127, pltpu.roll(t[4], 127, 1), last)
    main[q, own, 512:640] = jnp.where(lane < 64, t[2], tail).astype(BF16)
    column = jnp.sum(jnp.where(lane == 64, t[2], 0.0), axis=1, keepdims=True)
    extra[own] = jnp.where(lane == q, column, extra[own].astype(F32)).astype(BF16)


def dft_group(g, table, folded, perm_ref, fields, y_ref, lanes):
    x = fields[pl.ds(g * 6, 6)].astype(F32)
    low = x[:, :, : LON // 2].reshape(240, LON // 2)
    high = x[:, :, LON // 2 :].reshape(240, LON // 2)
    parts = []
    for par in range(2):
        x = low + high if par == 0 else low - high
        folded[0:120] = x[0:120].astype(BF16)
        folded[128:248] = x[120:240].astype(BF16)
        y = lax.dot_general(
            table[768 * par : 768 * par + 768], folded[...], NT, preferred_element_type=F32
        )
        y = jnp.dot(y.astype(BF16), perm_ref[...], preferred_element_type=F32)
        parts.append(y.reshape(NLAT, 24, 256))
    y_ref[:, :, lanes] = jnp.concatenate(parts, axis=1).astype(BF16)


def gather_lanes(pieces, width, offset, tile, lane):
    first, last = 128 * tile // width, min((128 * tile + 127) // width, len(pieces) - 1)
    total = None
    for l in range(first, last + 1):
        turned = pltpu.roll(pieces[l](), (width * l - offset) % 128, 1)
        start = width * l - 128 * tile
        total = turned if total is None else jnp.where(lane >= start, turned, total)
    return total


def strided(ref, lead, tiles, first, count, step):
    parts = [ref[lead, k, pl.ds(first, count, stride=step), :] for k in range(tiles)]
    return jnp.concatenate(parts, axis=1)


def fold_fields(ft, x_ref, folded, wide):
    half = NLAT // 2
    lane = lax.broadcasted_iota(jnp.int32, (48, 128), 1)
    lanes = pl.ds(pl.multiple_of(ft * 128, 128), 128)
    for l in range(half):
        n = x_ref[l, :, lanes].astype(F32)
        s = x_ref[NLAT - 1 - l, :, lanes].astype(F32)
        folded[0, l] = n + s
        folded[1, l] = n - s
    for sign in range(2):
        pieces = [lambda l=l: folded[sign, l] for l in range(half)]
        for tile in range(5):
            for fi in range(3):
                value = gather_lanes(pieces, ROWS, ROWS * fi, tile, lane)
                first = pl.multiple_of((3 * ft + fi) * 48, 8)
                wide[sign, tile, pl.ds(first, 48), :] = value


def legendre_pair(q, wide, main, extra, masks, synths, joined, levels):
    def operand(sign):
        parts = []
        for par in range(2):
            for c in range(2):
                parts.append(strided(wide, sign, 5, 24 * par + 2 * q + c, FLD, 48))
        return jnp.concatenate(parts, axis=0).astype(BF16)

    sym, anti = operand(0), operand(1)
    lane96 = lax.broadcasted_iota(jnp.int32, (96, 128), 1)
    z_sym = jnp.dot(sym, main[q, :, 0:256], preferred_element_type=F32)
    z_anti = jnp.dot(anti, main[q, :, 256:512], preferred_element_type=F32)
    tail = main[q, :, 512:640]
    z_tail = jnp.where(
        lane96 < 64,
        jnp.dot(sym, tail, preferred_element_type=F32),
        jnp.dot(anti, tail, preferred_element_type=F32),
    )
    z_extra = jnp.dot(sym, extra[...], preferred_element_type=F32)
    z_extra = jnp.sum(jnp.where(lane96 == q, z_extra, 0.0), axis=1, keepdims=True)
    mask = masks[q]

    def choose(z, row, first):
        even_first = mask[row : row + 1, first : first + z.shape[1]] > 0.5
        return jnp.where(even_first, z[0:48], z[48:96])

    z_sym = choose(z_sym, 0, 0).astype(BF16)
    z_anti = choose(z_anti, 0, 256).astype(BF16)
    z_tail = choose(z_tail, 0, 512).astype(BF16).astype(F32)
    z_extra = choose(jnp.broadcast_to(z_extra, (96, 128)), 1, 0)
    lane = lax.broadcasted_iota(jnp.int32, (48, 128), 1)
    sym32, anti32 = z_sym.astype(F32), z_anti.astype(F32)
    low, high = pltpu.roll(anti32[:, 0:128], 65, 1), pltpu.roll(anti32[:, 128:256], 65, 1)
    end = pltpu.roll(z_tail, 1, 1)
    own = pl.ds(pl.multiple_of(q * 48, 48), 48)
    joined[0, 0, own] = sym32[:, 0:128]
    joined[0, 1, own] = sym32[:, 128:256]
    joined[0, 2, own] = jnp.where(lane < 64, z_tail, jnp.where(lane == 64, z_extra, low))
    joined[0, 3, own] = jnp.where(lane < 65, low, high)
    joined[0, 4, own] = jnp.where(lane < 65, high, end)
    joined[0, 5, own] = end

    zero = jnp.zeros((), BF16)
    for level, place in enumerate((0, 3, 5)):
        size = LEVELS[level]
        h = size // 2
        keep = mask[2 + level : 3 + level]
        kept_sym = jnp.where(keep[:, 0:h] > 0.5, z_sym[:, 0:h], zero)
        kept_anti = jnp.where(keep[:, 256 : 256 + h] > 0.5, z_anti[:, 0:h], zero)
        even = jnp.dot(kept_sym, synths[level][q, 0], preferred_element_type=F32)
        odd = jnp.dot(kept_anti, synths[level][q, 1], preferred_element_type=F32)
        for sign, value in enumerate((even + odd, even - odd)):
            for k in range(0, size, 128):
                width = min(128, size - k)
                levels[sign, place + k // 128, own, 0:width] = value[:, k : k + width]


def turn_levels(levels, turned, blocks):
    half = NLAT // 2
    row = lax.broadcasted_iota(jnp.int32, (640, 1), 0).astype(F32)
    lane_of = lax.broadcasted_iota(jnp.int32, (640, 768), 1).astype(F32)
    block = jnp.floor((row + 0.5) * (1.0 / 40))
    t = row - 40.0 * block
    for sign in range(2):
        for f in range(FLD):
            first = 128 * (f // 6) + 20 * (f % 6)
            turned[first : first + 20] = strided(levels, sign, 6, f, 2 * PAIR, FLD)
        at = [t, t - 24.0, t - 34.0]
        if sign == 1:
            at = [19.0 - t, 33.0 - t, 38.0 - t]
        target = jnp.where(
            t < 20.0,
            20.0 * block + at[0],
            jnp.where(
                (t >= 24.0) & (t < 34.0),
                384.0 + 10.0 * block + at[1],
                jnp.where((t >= 34.0) & (t < 39.0), 640.0 + 5.0 * block + at[2], -1.0),
            ),
        )
        picker = jnp.where(lane_of == target, 1.0, 0.0).astype(BF16)
        picked = lax.dot_general(picker, turned[...].astype(BF16), NT, preferred_element_type=F32)
        picked = picked.reshape(half, 40, 512).astype(BF16)
        if sign == 0:
            blocks[0:half] = picked
        else:
            for m in range(half):
                blocks[NLAT - 1 - m] = picked[m]


def main_kernel(
    cols, icols, perm, masks, fields_in, legendre_in, s1_in, s2_in, s3_in,
    spec_out, blocks_out, t1_out, t2_out, t3_out,
    raw, main, extra, table, fields, folded_rows, y, x, folded, wide, joined, levels, turned,
    spec, blocks, s1, s2, s3, t1, t2, t3,
    raw_sem, field_sem, load_sem, store_sem, y_send, y_recv, near_send, near_recv,
    far_send, far_recv, extra_send, extra_recv, block_send, block_recv,
):
    lat = lax.axis_index("lat")
    fld = lax.axis_index("fld")
    rows = legendre_in.shape[1]
    own = pl.ds(pl.multiple_of(fld * rows, rows), rows)
    synths = (s1, s2, s3)

    def raw_copy(q):
        return pltpu.make_async_copy(legendre_in.at[q], raw.at[q], raw_sem.at[q])

    def field_copy(g):
        part = pl.ds(g * 6, 6)
        return pltpu.make_async_copy(fields_in.at[part], fields.at[part], field_sem.at[g])

    loads = [
        pltpu.make_async_copy(a, b, load_sem.at[k])
        for k, (a, b) in enumerate(((s1_in, s1), (s2_in, s2), (s3_in, s3)))
    ]
    tables = [
        pltpu.make_async_copy(a, b, store_sem.at[k])
        for k, (a, b) in enumerate(((t1, t1_out), (t2, t2_out), (t3, t3_out)))
    ]
    each(0, PAIR, lambda q: raw_copy(q).start())
    each(0, 4, lambda g: field_copy(g).start())
    for copy in loads:
        copy.start()
    extra[...] = jnp.zeros_like(extra)
    levels[...] = jnp.zeros_like(levels)
    turned[...] = jnp.zeros_like(turned)
    folded_rows[...] = jnp.zeros_like(folded_rows)
    greet()

    def shard(q, k):
        s = lax.rem(fld + k, NFLD)
        return main.at[q, pl.ds(pl.multiple_of(s * rows, rows), rows)]

    step = (1, NFLD - 1)

    def near(q, way):
        return to_fld(shard(q, 0), near_send.at[way, q], near_recv.at[way, q], step[way])

    def far(q, way):
        return to_fld(shard(q, step[1 - way]), far_send.at[q], far_recv.at[q], step[way])

    def extra_copy(k):
        return to_fld(extra.at[own], extra_send.at[k - 1], extra_recv.at[k - 1], k)

    def start_near(q):
        near(q, 0).start()
        near(q, 1).start()

    def pack_one(q):
        raw_copy(q).wait()
        pack_pair(q, raw, main, extra, own)

    pack_one(0)
    pack_one(1)
    start_near(0)

    def fill(b):
        first = pl.multiple_of(b * 64, 64)

        def store(a, value):
            table[pl.ds(first, 64), 128 * a : 128 * a + 128] = value.astype(BF16)

        fill_table(cols, first, 64, LON, 1.0 / math.sqrt(LON), 10, store)

    each(0, 24, fill)
    start_near(1)

    def lanes_of(g):
        return pl.ds(pl.multiple_of(g * 256, 256), 256)

    def y_copy(g, k):
        return to_lat(
            y.at[lat_peer(k), :, lanes_of(g)],
            x.at[lat, :, lanes_of(g)],
            y_send.at[g, k - 1],
            y_recv.at[g, k - 1],
            k,
        )

    def group(g):
        field_copy(g).wait()
        dft_group(g, table, folded_rows, perm, fields, y, lanes_of(g))
        x[lat, :, lanes_of(g)] = y[lat, :, lanes_of(g)]
        pack_one(2 * g + 2)
        pack_one(2 * g + 3)
        each(1, NLAT, lambda k: y_copy(g, k).start())
        start_near(2 * g + 2)
        start_near(2 * g + 3)

    each(0, 4, group)
    for k in range(1, NFLD):
        extra_copy(k).start()

    def fill_inverse(b):
        first = pl.multiple_of(b * 64, 64)
        for out, size, tiles in ((t1, 1280, 10), (t2, 640, 5), (t3, 320, 3)):

            def store(a, value, out=out):
                out[pl.ds(first, 64), 128 * a : 128 * a + 128] = value.astype(BF16)

            fill_table(icols, first, 64, size, 1.0 / math.sqrt(size), tiles, store)

    each(0, 10, fill_inverse)

    def relay(h):
        near(2 * h, 0).wait_recv()
        far(2 * h, 0).start()
        near(2 * h + 1, 1).wait_recv()
        far(2 * h + 1, 1).start()

    each(0, PAIR // 2, relay)
    for copy in tables:
        copy.start()
    for copy in loads:
        copy.wait()
    for k in range(1, NFLD):
        extra_copy(k).wait()

    def arrived(g):
        each(1, NLAT, lambda k: y_copy(g, k).wait())
        fold_fields(2 * g, x, folded, wide)
        fold_fields(2 * g + 1, x, folded, wide)

    each(0, 4, arrived)

    def pairs(h):
        near(2 * h, 1).wait_recv()
        far(2 * h, 0).wait_recv()
        legendre_pair(2 * h, wide, main, extra, masks, synths, joined, levels)
        near(2 * h + 1, 0).wait_recv()
        far(2 * h + 1, 1).wait_recv()
        legendre_pair(2 * h + 1, wide, main, extra, masks, synths, joined, levels)

    each(0, PAIR // 2, pairs)
    turn_levels(levels, turned, blocks)

    def block_copy(k):
        return to_lat(
            blocks.at[lat_peer(k)],
            blocks_out.at[lat],
            block_send.at[k - 1],
            block_recv.at[k - 1],
            k,
        )

    each(1, NLAT, lambda k: block_copy(k).start())
    own_block = pltpu.make_async_copy(blocks.at[lat], blocks_out.at[lat], store_sem.at[3])
    own_block.start()

    def field(f):
        part = strided(joined, 0, 6, f, 2 * PAIR, FLD)
        spec[f] = part[:, 0:641].reshape(PAIR, 2, 641).astype(BF16)

    each(0, FLD, field)
    spec_copy = pltpu.make_async_copy(spec, spec_out, store_sem.at[4])
    spec_copy.start()

    def sent(h):
        for way in range(2):
            near(2 * h, way).wait_send()
            near(2 * h + 1, way).wait_send()
        far(2 * h, 0).wait_send()
        far(2 * h + 1, 1).wait_send()

    each(0, PAIR // 2, sent)
    for copy in tables:
        copy.wait()
    each(1, NLAT, lambda k: block_copy(k).wait())
    own_block.wait()
    spec_copy.wait()


def main_step(cols, icols, perm, masks, fields, legendre_t, synths):
    hbm = pl.BlockSpec(memory_space=pltpu.HBM)
    vmem = pl.BlockSpec(memory_space=pltpu.VMEM)
    dma = pltpu.SemaphoreType.DMA
    rows = legendre_t.shape[1]
    synths = [s.reshape(PAIR, 2, m // 2, m) for s, m in zip(synths, LEVELS)]
    wides = (1280, 640, 384)
    return pl.pallas_call(
        main_kernel,
        in_specs=[vmem] * 4 + [hbm] * 5,
        out_specs=[hbm] * 5,
        out_shape=[
            jax.ShapeDtypeStruct((FLD, PAIR, 2, 641), BF16),
            jax.ShapeDtypeStruct((NLAT, 40, 512), BF16),
            *[jax.ShapeDtypeStruct((640, w), BF16) for w in wides],
        ],
        scratch_shapes=[
            pltpu.VMEM((PAIR, rows, 641), BF16),
            pltpu.VMEM((PAIR, NFLD * rows, 640), BF16),
            pltpu.VMEM((NFLD * rows, 128), BF16),
            pltpu.VMEM((1536, LON // 2), BF16),
            pltpu.VMEM((FLD, ROWS, LON), BF16),
            pltpu.VMEM((256, LON // 2), BF16),
            pltpu.VMEM((NLAT, 48, 1024), BF16),
            pltpu.VMEM((NLAT, 48, 1024), BF16),
            pltpu.VMEM((2, NLAT // 2, 48, 128), F32),
            pltpu.VMEM((2, 5, 48 * FLD, 128), F32),
            pltpu.VMEM((1, 6, 48 * PAIR, 128), F32),
            pltpu.VMEM((2, 6, 48 * PAIR, 128), F32),
            pltpu.VMEM((512, 768), F32),
            pltpu.VMEM((FLD, PAIR, 2, 641), BF16),
            pltpu.VMEM((NLAT, 40, 512), BF16),
            *[pltpu.VMEM(s.shape, BF16) for s in synths],
            *[pltpu.VMEM((640, w), BF16) for w in wides],
            dma((PAIR,)), dma((4,)), dma((3,)), dma((5,)),
            dma((4, NLAT - 1)), dma((4, NLAT - 1)),
            dma((2, PAIR)), dma((2, PAIR)), dma((PAIR,)), dma((PAIR,)),
            dma((NFLD - 1,)), dma((NFLD - 1,)),
            dma((NLAT - 1,)), dma((NLAT - 1,)),
        ],
        compiler_params=pltpu.CompilerParams(
            collective_id=0, has_side_effects=True, vmem_limit_bytes=64 * 1000 * 1000
        ),
    )(cols, icols, perm, masks, fields, legendre_t, *synths)


def inverse_kernel(b_ref, t1, t2, t3, o1_ref, o2_ref, o3_ref, wide):
    lane = lax.broadcasted_iota(jnp.int32, (40, 128), 1)

    def group(g, carry):
        lanes = pl.ds(pl.multiple_of(g * 128, 128), 128)
        pieces = [lambda l=l: b_ref[l, :, lanes].astype(F32) for l in range(NLAT)]
        for tile in range(5):
            for fi in range(6):
                value = gather_lanes(pieces, 20, 20 * fi, tile, lane)
                first = pl.multiple_of((6 * g + fi) * 40, 8)
                wide[0, tile, pl.ds(first, 40), :] = value
        return carry

    lax.fori_loop(0, 4, group, 0)
    for out_ref, table, start, count in (
        (o1_ref, t1, 0, 20), (o2_ref, t2, 24, 10), (o3_ref, t3, 34, 5)
    ):
        parts = [strided(wide, 0, 5, start + t, FLD, 40) for t in range(count)]
        lhs = jnp.concatenate(parts, axis=0).astype(BF16)
        size = out_ref.shape[2]
        y = jnp.dot(lhs, table[...], preferred_element_type=F32)
        out_ref[...] = y[:, 0:size].reshape(count, FLD, size)


def inverse_step(blocks, tables):
    shapes = [(n, FLD, 4 * m) for n, m in zip(SENT, LEVELS)]
    return pl.pallas_call(
        inverse_kernel,
        in_specs=[pl.BlockSpec(memory_space=pltpu.VMEM)] * 4,
        out_specs=[pl.BlockSpec(memory_space=pltpu.VMEM)] * 3,
        out_shape=[jax.ShapeDtypeStruct(s, F32) for s in shapes],
        scratch_shapes=[
            pltpu.VMEM((1, 5, 40 * FLD, 128), F32),
        ],
    )(blocks, *tables)


def columns(wave, amp, comp):
    parts = [jnp.broadcast_to(v, wave.shape).astype(F32) for v in (wave, amp, comp)]
    return jnp.pad(jnp.stack(parts, axis=-1), ((0, 0), (0, 5)))


def forward_columns(assign):
    even = jnp.where(assign % 2 == 0, assign, 2 * assign.shape[0] - 1 - assign)
    wave = jnp.stack([even, 2 * assign.shape[0] - 1 - even])
    wave = jnp.repeat(wave.reshape(2, NLAT, PAIR), 2, axis=2)
    wave = jnp.pad(wave, ((0, 0), (0, 0), (0, 4))).reshape(-1)
    place = jnp.arange(wave.shape[0]) % 24
    return columns(wave, place < 20, place % 2)


def inverse_columns(assign):
    wave = jnp.repeat(assign, 2)
    return columns(wave, jnp.where(wave == 0, 1.0, 2.0), jnp.arange(wave.shape[0]) % 2)


def mask_rows(own, limits):
    p = own[:, None]
    total = 640
    k = jnp.arange(256)[None, :]
    tail = jnp.arange(64)[None, :] + 256
    first_sym, first_anti = (total + 1 - p) // 2, (total - p) // 2
    zeroth = jnp.concatenate(
        [k < first_sym, k < first_anti, tail < first_sym, tail < first_anti], axis=1
    )
    is_even = p % 2 == 0
    row0 = zeroth == is_even
    row1 = jnp.broadcast_to((320 < first_sym) == is_even, row0.shape)
    rows = [row0, row1]
    for level in range(3):
        keep = [p + 2 * k <= limits[level], p + 1 + 2 * k <= limits[level]]
        rows.append(jnp.concatenate(keep + [jnp.zeros((PAIR, 128), bool)], axis=1))
    stacked = jnp.stack(rows, axis=1).astype(F32)
    return jnp.pad(stacked, ((0, 0), (0, 3), (0, 0)))


def row_turner(lat):
    u = jnp.arange(256)[:, None]
    v = jnp.arange(256)[None, :]
    inner = v % 128
    turned = 128 * (v // 128) + 40 * (inner // 40) + 39 - inner % 40
    source = jnp.where(lat >= NLAT // 2, turned, v)
    return ((u == source) & (inner < 120)).astype(BF16)


def on_device(grid_fields, assign, limits, legendre, synth_one, synth_two, synth_three):
    lat = lax.axis_index("lat")
    own = lax.dynamic_slice_in_dim(assign, lat * PAIR, PAIR)
    spectrum, blocks, *tables = main_step(
        forward_columns(assign),
        inverse_columns(assign),
        row_turner(lat),
        mask_rows(own, limits),
        grid_fields,
        jnp.transpose(legendre, (0, 2, 1)),
        (synth_one, synth_two, synth_three),
    )
    grids = inverse_step(blocks, tables)
    return (
        jnp.transpose(spectrum, (0, 2, 1, 3)),
        *[jnp.transpose(g, (1, 0, 2)) for g in grids],
    )


def solution(mesh):
    return jax.shard_map(
        on_device,
        mesh=mesh,
        in_specs=(
            P("fld", "lat", None),
            P(),
            P(),
            P("lat", None, "fld"),
            P("lat", None, None),
            P("lat", None, None),
            P("lat", None, None),
        ),
        out_specs=(
            P("fld", None, "lat", None),
            P("fld", "lat", None),
            P("fld", "lat", None),
            P("fld", "lat", None),
        ),
        check_vma=False,
    )
```

profile of v0, /device:TPU:1, one launch (start us, length us, event | category | flops | bytes accessed | tf_op | source)
XLA Modules:
  0.0 124.7 jit_solution(3202487422602747115)
XLA Ops:
  0.7 0.8 broadcast_add_fusion
  1.5 1.4 %fusion.19 = (s32[1]{0:T(128)}, s32[1]{0:T(128)}, s32[1]{0:T(128)}) fusion(s32[3]{0:T(128)} %param.9), kind=kLoop, calls=%fused_computation.74 | loop fusion | bytes 24 | tf_op jit(solution)/shard_map/slice | solution.py:562
  2.9 0.7 compare_select_fusion.4
  3.6 0.1 compare_bitcast_fusion.1
  3.7 0.8 broadcast_subtract_fusion
  4.5 0.1 fusion.2
  4.6 0.1 pad_add_fusion
  4.6 0.1 stack.35
  4.7 0.1 copy.57
  4.8 0.1 copy_compare_fusion
  4.9 0.1 stack.34
  5.0 0.1 copy.56
  5.2 0.1 copy.59
  5.3 0.1 convert_element_type.68
  5.4 2.0 %add_compare_fusion.3 = (pred[10,256]{1,0:T(8,128)(4,1)S(1)}, pred[10,256]{1,0:T(8,128)(4,1)S(1)}, pred[10,256]{1,0:T(8,128)(4,1)S(1)}, pred[10,256]{1,0:T(8,128...) fusion(s32[]{:T(128)} %bitcast.9, s32[256]{0:T(256)S(1)} %iota_multiply_fusion, ...), kind=kLoop, calls=%fused_computation.12 | loop fusion | flops 20480 | bytes 16476 | tf_op jit(solution)/shard_map/le | solution.py:562
  7.5 0.1 stack_broadcast_in_dim.2
  7.7 0.2 stack.42
  7.9 0.7 fusion.1.perm
  8.6 0.7 pad_convert_fusion.masks
  9.3 0.1 broadcast_in_dim.25
  9.4 0.1 select_n.150
  9.5 0.1 broadcast_in_dim.22
  9.6 0.1 convert_element_type.72
  9.8 0.2 copy.61
  10.0 0.8 pad.20.icols
  10.7 0.3 copy.60
  11.0 0.9 pad.19.cols
  12.0 104.1 %shard_map.102 = (bf16[24,10,2,641]{3,2,1,0:T(2,128)(2,1)}, bf16[32,40,512]{2,1,0:T(8,128)(2,1)}, bf16[640,1280]{1,0:T(8,128)(2,1)}, bf16[640,640]{1,0:T(8,128)(2,1)}, bf16[640,384]{1,0:T(8,128)(2,1)}) custom-call(f32[1536,8]{1,0:T(8,128)} %pad.19.cols, f32[640,8]{1,0:T(8,128)} %pad.20.icols, bf16[256,256]{1,0:T(8,128)(2,1)} %fusion.1.perm, ...), custom_call_target="tpu_custom_call" | custom-call | tf_op jit(solution)/shard_map/pallas_call | solution.py:453
  116.1 0.0 copy-start
  116.1 7.8 %shard_map.103 = (f32[20,24,1280]{2,1,0:T(8,128)}, f32[10,24,640]{2,1,0:T(8,128)}, f32[5,24,320]{2,1,0:T(8,128)}) custom-call(bf16[32,40,512]{2,1,0:T(8,128)(2,1)} %get-tuple-element.13.b_ref, bf16[640,1280]{1,0:T(8,128)(2,1)} %get-tuple-element.14.t1, bf16[640,640]{1,0:T(8,128)(2,1)} %get-tuple-element.15.t2, bf16[640,384]{1,0:T(8,128)(2,1)} %get-tuple-element.16.t3), custom_call_target="tpu_custom_call" | custom-call | tf_op jit(solution)/shard_map/pallas_call | solution.py:518
  123.9 0.0 copy-done
  123.9 0.9 copy.68
  (21 shorter events, 0.3 us)
Async XLA Ops:
  116.1 7.8 %copy-start = (bf16[24,10,2,641]{3,2,1,0:T(2,128)(2,1)S(1)}, bf16[24,10,2,641]{3,2,1,0:T(2,128)(2,1)}, u32[]{:S(2)}) copy-start(bf16[24,10,2,641]{3,2,1,0:T(2,128)(2,1)} %get-tuple-element.12) | copy-start | bytes 1846084
where the time goes:
time: 127 us; the launch traced here: 125 us
  Pallas kernels  112 us (88%)
  other arithmetic  6.21 us (5%)
  local copies, waits for them, and re-layouts  5.79 us (5%)
    pallas_call x1, Pallas kernels, main_step(): pl.pallas_call(main_kernel, in_specs=[vmem] * 4 + [hbm] * 5, out_specs=[h...  104 us
    pallas_call x1, Pallas kernels, inverse_step(): pl.pallas_call(inverse_kernel, in_specs=[pl.BlockSpec(memory_space=pltpu....  7.78 us

commit v1 on v0

v1 whole, which is shorter than its diff:
```python
import math

import jax
import jax.numpy as jnp
from jax import lax
from jax.experimental import pallas as pl
from jax.experimental.pallas import tpu as pltpu
from jax.sharding import PartitionSpec as P

MESH = pl.DeviceIdType.MESH
F32 = jnp.float32
BF16 = jnp.bfloat16
NLAT = 32
NFLD = 4
FLD = 24
ROWS = 40
LON = 2560
PAIR = 10
SENT = (20, 10, 5)
LEVELS = (320, 160, 80)
NT = (((1,), (1,)), ((), ()))
EARLY = 8
DEEP = 2 * EARLY * NLAT


def sincos(turns):
    quarter = jnp.floor(turns * 4.0 + 0.5)
    y = (turns * 4.0 - quarter) * (math.pi / 2)
    y2 = y * y
    s = y * (1.0 + y2 * (-1.0 / 6 + y2 * (1.0 / 120 - y2 * (1.0 / 5040))))
    c = 1.0 + y2 * (-0.5 + y2 * (1.0 / 24 + y2 * (-1.0 / 720 + y2 * (1.0 / 40320))))
    k = quarter - 4.0 * jnp.floor(quarter * 0.25)
    odd = (k == 1.0) | (k == 3.0)
    sin_v = jnp.where(odd, c, s)
    cos_v = jnp.where(odd, s, c)
    sin_v = jnp.where(k >= 2.0, -sin_v, sin_v)
    cos_v = jnp.where((k == 1.0) | (k == 2.0), -cos_v, cos_v)
    return cos_v, sin_v


def turns_of(product, period):
    return (product - period * jnp.floor(product * (1.0 / period))) * (1.0 / period)


def fill_table(cols_ref, first, count, period, scale, tiles, store):
    wave = jnp.broadcast_to(cols_ref[pl.ds(first, count), 0:1], (count, 128))
    amp = jnp.broadcast_to(cols_ref[pl.ds(first, count), 1:2], (count, 128)) * scale
    comp = jnp.broadcast_to(cols_ref[pl.ds(first, count), 2:3], (count, 128))
    lane = lax.broadcasted_iota(jnp.int32, (count, 128), 1).astype(F32)
    cos_v, sin_v = sincos(turns_of(wave * lane + comp * (period // 4), float(period)))
    cos_d, sin_d = sincos(turns_of(wave * 128.0, float(period)))
    cos_v, sin_v = cos_v * amp, sin_v * amp
    for a in range(tiles):
        store(a, cos_v)
        if a + 1 < tiles:
            cos_v, sin_v = cos_v * cos_d - sin_v * sin_d, sin_v * cos_d + cos_v * sin_d


def lat_peer(k):
    return lax.rem(lax.axis_index("lat") + k, NLAT)


def greet():
    barrier = pltpu.get_barrier_semaphore()
    fld = lax.axis_index("fld")
    lat = lax.axis_index("lat")

    def one(k, carry):
        pl.semaphore_signal(barrier, inc=1, device_id=(lat_peer(k), fld), device_id_type=MESH)
        return carry

    lax.fori_loop(1, NLAT, one, 0)
    for k in range(1, NFLD):
        pl.semaphore_signal(
            barrier, inc=1, device_id=(lat, lax.rem(fld + k, NFLD)), device_id_type=MESH
        )
    return lambda: pl.semaphore_wait(barrier, NLAT + NFLD - 2)


def to_lat(src, dst, send_sem, recv_sem, k):
    return pltpu.make_async_remote_copy(
        src_ref=src,
        dst_ref=dst,
        send_sem=send_sem,
        recv_sem=recv_sem,
        device_id=(lat_peer(k), lax.axis_index("fld")),
        device_id_type=MESH,
    )


def to_fld(part, send_sem, recv_sem, k):
    fld = lax.rem(lax.axis_index("fld") + k, NFLD)
    return pltpu.make_async_remote_copy(
        src_ref=part,
        dst_ref=part,
        send_sem=send_sem,
        recv_sem=recv_sem,
        device_id=(lax.axis_index("lat"), fld),
        device_id_type=MESH,
    )


def each(first, count, act):
    def one(k, carry):
        act(k)
        return carry

    lax.fori_loop(first, count, one, 0)


def pack_pair(q, raw, main, extra, own):
    a = raw[q].astype(F32)
    t = [a[:, 128 * k : 128 * k + 128] for k in range(5)]
    last = a[:, 640:641]
    lane = lax.broadcasted_iota(jnp.int32, (a.shape[0], 128), 1)
    r = [None, None] + [pltpu.roll(t[k], 63, 1) for k in (2, 3, 4)]
    main[q, own, 0:128] = t[0].astype(BF16)
    main[q, own, 128:256] = t[1].astype(BF16)
    main[q, own, 256:384] = jnp.where(lane < 63, r[2], r[3]).astype(BF16)
    main[q, own, 384:512] = jnp.where(lane < 63, r[3], r[4]).astype(BF16)
    tail = jnp.where(lane < 127, pltpu.roll(t[4], 127, 1), last)
    main[q, own, 512:640] = jnp.where(lane < 64, t[2], tail).astype(BF16)
    column = jnp.sum(jnp.where(lane == 64, t[2], 0.0), axis=1, keepdims=True)
    extra[own] = jnp.where(lane == q, column, extra[own].astype(F32)).astype(BF16)


def dft_group(g, table, folded, perm_ref, fields, y_ref, lanes):
    x = fields[pl.ds(g * 6, 6)].astype(F32)
    low = x[:, :, : LON // 2].reshape(240, LON // 2)
    high = x[:, :, LON // 2 :].reshape(240, LON // 2)
    parts = []
    for par in range(2):
        x = low + high if par == 0 else low - high
        folded[0:120] = x[0:120].astype(BF16)
        folded[128:248] = x[120:240].astype(BF16)
        y = lax.dot_general(
            table[768 * par : 768 * par + 768], folded[...], NT, preferred_element_type=F32
        )
        y = jnp.dot(y.astype(BF16), perm_ref[...], preferred_element_type=F32)
        parts.append((y[0:512].reshape(NLAT, 16, 256), y[512:768].reshape(NLAT, 8, 256)))
    (first, mid), (last, other) = parts
    y_ref[:, :, lanes] = jnp.concatenate([first, mid + other, last], axis=1).astype(BF16)


def make_columns(assign_ref, cols, part):
    p = assign_ref[...].reshape(1, -1).astype(F32)
    total = 2.0 * assign_ref.shape[0] - 1.0
    even = jnp.where(p - 2.0 * jnp.floor(p * 0.5) > 0.5, total - p, p)
    value = (even, total - even, p)[part]
    high = jnp.floor(value * (1.0 / 16))
    place = lax.broadcasted_iota(jnp.int32, (8, value.shape[1]), 0)
    digits = jnp.where(place == 0, high, jnp.where(place == 1, value - 16.0 * high, 0.0))
    r = lax.broadcasted_iota(jnp.int32, (768, 1), 0).astype(F32)
    if part < 2:
        rest = r >= 512.0
        s = jnp.where(rest, r - 512.0, r)
        l = jnp.where(rest, jnp.floor((s + 0.5) * (1.0 / 8)), jnp.floor((s + 0.5) * (1.0 / 16)))
        i = s - jnp.where(rest, 8.0, 16.0) * l
        if part == 0:
            valid = jnp.logical_not(rest) | (i < 4.0)
            q = jnp.floor(i * 0.5) + jnp.where(rest, 8.0, 0.0)
        else:
            valid = jnp.logical_not(rest) | (i >= 4.0)
            q = jnp.floor(i * 0.5) + jnp.where(rest, 6.0, 0.0)
    else:
        late = r >= 512.0
        s = jnp.where(late, r - 512.0, r)
        valid = r < 640.0
        l = jnp.where(late, jnp.floor((s + 0.5) * 0.25), jnp.floor((s + 0.5) * (1.0 / 16)))
        i = s - jnp.where(late, 4.0, 16.0) * l
        q = jnp.floor(i * 0.5) + jnp.where(late, 8.0, 0.0)
    slot = jnp.where(valid, 10.0 * l + q, -1.0)
    lane = lax.broadcasted_iota(jnp.int32, (768, value.shape[1]), 1).astype(F32)
    picker = jnp.where(lane == slot, 1.0, 0.0).astype(BF16)
    found = lax.dot_general(picker, digits.astype(BF16), NT, preferred_element_type=F32)
    wave = 16.0 * found[:, 0:1] + found[:, 1:2]
    amp = jnp.where(valid, 1.0, 0.0)
    if part == 2:
        amp = amp * jnp.where(wave > 0.5, 2.0, 1.0)
    rows = slice(768 * part, 768 * part + 768)
    cols[rows, 0:1] = wave
    cols[rows, 1:2] = amp
    cols[rows, 2:3] = r - 2.0 * jnp.floor(r * 0.5)


def make_turner(perm):
    u = lax.broadcasted_iota(jnp.int32, (256, 256), 0).astype(F32)
    v = lax.broadcasted_iota(jnp.int32, (256, 256), 1).astype(F32)
    inner = v - 128.0 * jnp.floor(v * (1.0 / 128))
    t = inner - 40.0 * jnp.floor((inner + 0.5) * (1.0 / 40))
    source = jnp.where(lax.axis_index("lat") >= NLAT // 2, v + 39.0 - 2.0 * t, v)
    perm[...] = jnp.where((u == source) & (inner < 120.0), 1.0, 0.0).astype(BF16)


def gather_lanes(pieces, width, offset, tile, lane):
    first, last = 128 * tile // width, min((128 * tile + 127) // width, len(pieces) - 1)
    total = None
    for l in range(first, last + 1):
        turned = pltpu.roll(pieces[l](), (width * l - offset) % 128, 1)
        start = width * l - 128 * tile
        total = turned if total is None else jnp.where(lane >= start, turned, total)
    return total


def strided(ref, lead, tiles, first, count, step):
    parts = [ref[lead + k, pl.ds(first, count, stride=step), :] for k in range(tiles)]
    return jnp.concatenate(parts, axis=1)


def fold_fields(ft, x_ref, folded, wide):
    half = NLAT // 2
    lane = lax.broadcasted_iota(jnp.int32, (40, 128), 1)
    lanes = pl.ds(pl.multiple_of(ft * 128, 128), 128)
    for l in range(half):
        n = x_ref[l, :, lanes].astype(F32)
        s = x_ref[NLAT - 1 - l, :, lanes].astype(F32)
        folded[0, l] = n + s
        folded[1, l] = n - s
    for sign in range(2):
        pieces = [lambda l=l: folded[sign, l] for l in range(half)]
        for tile in range(5):
            for fi in range(3):
                value = gather_lanes(pieces, ROWS, ROWS * fi, tile, lane)
                first = pl.multiple_of((3 * ft + fi) * 40, 8)
                wide[5 * sign + tile, pl.ds(first, 40), :] = value


def legendre_pair(q, p, limits, wide, main, extra, synths, joined, levels):
    def operand(sign):
        parts = []
        for par in range(2):
            for c in range(2):
                row = 2 * q + c
                if par == 1:
                    row += 24 - 20 * lax.div(q, 8)
                parts.append(strided(wide, 5 * sign, 5, row, FLD, 40))
        return jnp.concatenate(parts, axis=0).astype(BF16)

    sym, anti = operand(0), operand(1)
    lane96 = lax.broadcasted_iota(jnp.int32, (96, 128), 1)
    z_sym = jnp.dot(sym, main[q, :, 0:256], preferred_element_type=F32)
    z_anti = jnp.dot(anti, main[q, :, 256:512], preferred_element_type=F32)
    tail = main[q, :, 512:640]
    z_tail = jnp.where(
        lane96 < 64,
        jnp.dot(sym, tail, preferred_element_type=F32),
        jnp.dot(anti, tail, preferred_element_type=F32),
    )
    z_extra = jnp.dot(sym, extra[...], preferred_element_type=F32)
    z_extra = jnp.sum(jnp.where(lane96 == q, z_extra, 0.0), axis=1, keepdims=True)
    first_sym = lax.shift_right_logical(641 - p, 1)
    first_anti = lax.shift_right_logical(640 - p, 1)
    parity = lax.bitwise_and(p, 1)

    def choose(z, rank, first):
        taken = jnp.where(rank < first, 1, 0) ^ parity
        return jnp.where(taken == 1, z[0:48], z[48:96])

    lane = lax.broadcasted_iota(jnp.int32, (48, 128), 1)
    rank = lax.broadcasted_iota(jnp.int32, (48, 256), 1)
    z_sym = choose(z_sym, rank, first_sym).astype(BF16)
    z_anti = choose(z_anti, rank, first_anti).astype(BF16)
    z_tail = jnp.where(
        lane < 64,
        choose(z_tail, lane + 256, first_sym),
        choose(z_tail, lane + 192, first_anti),
    )
    z_tail = z_tail.astype(BF16).astype(F32)
    z_extra = choose(jnp.broadcast_to(z_extra, (96, 128)), lane * 0 + 320, first_sym)
    sym32, anti32 = z_sym.astype(F32), z_anti.astype(F32)
    low, high = pltpu.roll(anti32[:, 0:128], 65, 1), pltpu.roll(anti32[:, 128:256], 65, 1)
    end = pltpu.roll(z_tail, 1, 1)
    own = pl.ds(pl.multiple_of(q * 48, 48), 48)
    joined[0, own] = sym32[:, 0:128]
    joined[1, own] = sym32[:, 128:256]
    joined[2, own] = jnp.where(lane < 64, z_tail, jnp.where(lane == 64, z_extra, low))
    joined[3, own] = jnp.where(lane < 65, low, high)
    joined[4, own] = jnp.where(lane < 65, high, end)
    joined[5, own] = end

    for level, place in enumerate((0, 3, 5)):
        size = LEVELS[level]
        h = size // 2
        degree = p + 2 * rank
        kept_sym = jnp.where(degree <= limits[level], sym32, 0.0).astype(BF16)[:, 0:h]
        kept_anti = jnp.where(degree + 1 <= limits[level], anti32, 0.0).astype(BF16)[:, 0:h]
        even = jnp.dot(kept_sym, synths[level][q, 0], preferred_element_type=F32)
        odd = jnp.dot(kept_anti, synths[level][q, 1], preferred_element_type=F32)
        for sign, value in enumerate((even + odd, even - odd)):
            for k in range(0, size, 128):
                width = min(128, size - k)
                levels[6 * sign + place + k // 128, own, 0:width] = value[:, k : k + width]


def make_pickers(pickers):
    row = lax.broadcasted_iota(jnp.int32, (640, 1), 0).astype(F32)
    lane_of = lax.broadcasted_iota(jnp.int32, (640, 768), 1).astype(F32)
    block = jnp.floor((row + 0.5) * (1.0 / 40))
    t = row - 40.0 * block
    for sign in range(2):
        at = [t, t - 24.0, t - 34.0]
        if sign == 1:
            at = [19.0 - t, 33.0 - t, 38.0 - t]
        target = jnp.where(
            t < 20.0,
            20.0 * block + at[0],
            jnp.where(
                (t >= 24.0) & (t < 34.0),
                384.0 + 10.0 * block + at[1],
                jnp.where((t >= 34.0) & (t < 39.0), 640.0 + 5.0 * block + at[2], -1.0),
            ),
        )
        pickers[sign] = jnp.where(lane_of == target, 1.0, 0.0).astype(BF16)


def turn_levels(part, levels, turned, pickers, blocks):
    half = NLAT // 2
    count = 2 * (EARLY if part == 0 else PAIR - EARLY)
    base = 0 if part == 0 else 2 * EARLY * FLD
    size = blocks.shape[2]
    for sign in range(2):
        for f in range(FLD):
            value = strided(levels, 6 * sign, 6, base + f, count, FLD)
            turned[base + count * f : base + count * f + count] = value
        picked = lax.dot_general(
            pickers[sign],
            turned[base : base + size].astype(BF16),
            NT,
            preferred_element_type=F32,
        )
        picked = picked.reshape(half, 40, size).astype(BF16)
        if sign == 0:
            blocks[0:half] = picked
        else:
            for m in range(half):
                blocks[NLAT - 1 - m] = picked[m]


def swap_units(values, width):
    lane = lax.broadcasted_iota(jnp.int32, values[0].shape, 1)
    values = list(values)
    k = 1
    while k < len(values):
        upper = (lane & (k * width)) != 0
        for a in range(len(values)):
            if a & k == 0:
                low, high = values[a], values[a + k]
                values[a] = jnp.where(upper, pltpu.roll(high, k * width, 1), low)
                values[a + k] = jnp.where(upper, high, pltpu.roll(low, 128 - k * width, 1))
        k *= 2
    return values


def spread_early(arrived, wide):
    def group(g):
        lanes = pl.ds(pl.multiple_of(g * 128, 128), 128)
        for tile in range(4):
            values = [arrived[8 * tile + a, :, lanes].astype(F32) for a in range(8)]
            for a, value in enumerate(swap_units(values, 16)):
                wide[tile, pl.ds(8 * g + a, 40, stride=FLD), :] = value

    each(0, 3, group)


def spread_late(arrived, wide):
    def rows(b):
        own = pl.ds(pl.multiple_of(8 * b, 8), 8)
        values = [arrived[l, own, :].astype(F32) for l in range(NLAT)]
        for f, value in enumerate(swap_units(values, 4)[0:FLD]):
            wide[4, pl.ds(8 * FLD * b + f, 8, stride=FLD), :] = value

    each(0, 5, rows)


LEVEL_ROWS = ((0, 480), (576, 240), (816, 120))


def main_kernel(
    assign_s, limits, assign_v, fields_in, legendre_in, s1_in, s2_in, s3_in,
    spec_out, rows_out, p1_out, p2_out, p3_out, t1_out, t2_out, t3_out,
    raw, main, extra, table, fields, folded_rows, y, x, folded, wide, joined, levels, turned,
    spec, early, late, early_in, late_in, rows_v, pickers, cols, perm, s1, s2, s3, t1, t2, t3,
    p1, p2, p3,
    raw_sem, field_sem, load_sem, store_sem, y_send, y_recv, near_send, near_recv,
    far_send, far_recv, extra_send, extra_recv, block_send, block_recv,
):
    lat = lax.axis_index("lat")
    fld = lax.axis_index("fld")
    rows = legendre_in.shape[1]
    own = pl.ds(pl.multiple_of(fld * rows, rows), rows)
    synths = (s1, s2, s3)

    def raw_copy(q):
        return pltpu.make_async_copy(legendre_in.at[q], raw.at[q], raw_sem.at[q])

    def field_copy(g):
        part = pl.ds(g * 6, 6)
        return pltpu.make_async_copy(fields_in.at[part], fields.at[part], field_sem.at[g])

    loads = [
        pltpu.make_async_copy(a, b, load_sem.at[k])
        for k, (a, b) in enumerate(((s1_in, s1), (s2_in, s2), (s3_in, s3)))
    ]
    tables = [
        pltpu.make_async_copy(a.at[pl.ds(DEEP, 128)], b, store_sem.at[k])
        for k, (a, b) in enumerate(((t1, t1_out), (t2, t2_out), (t3, t3_out)))
    ]
    each(0, PAIR, lambda q: raw_copy(q).start())
    each(0, 4, lambda g: field_copy(g).start())
    for copy in loads:
        copy.start()
    all_greeted = greet()
    extra[own] = jnp.zeros((rows, 128), BF16)
    folded_rows[...] = jnp.zeros_like(folded_rows)

    def shard(q, k):
        s = lax.rem(fld + k, NFLD)
        return main.at[q, pl.ds(pl.multiple_of(s * rows, rows), rows)]

    def near(h, way):
        pair = main.at[pl.ds(2 * h, 2), own]
        return to_fld(pair, near_send, near_recv.at[way, h], 1 + 2 * way)

    def near_last(q, way):
        return to_fld(shard(q, 0), near_send, near_recv.at[way, q - 4], 1 + 2 * way)

    def far(q, way):
        return to_fld(shard(q, 3 - 2 * way), far_send, far_recv.at[q], 1 + 2 * way)

    def extra_copy(k):
        return to_fld(extra.at[own], extra_send.at[k - 1], extra_recv.at[k - 1], k)

    def start_near(h):
        near(h, 0).start()
        near(h, 1).start()

    def start_last():
        near_last(8, 0).start()
        near_last(9, 1).start()
        near_last(9, 0).start()
        near_last(8, 1).start()

    def pack_one(q):
        raw_copy(q).wait()
        pack_pair(q, raw, main, extra, own)

    pack_one(0)
    pack_one(1)
    all_greeted()
    start_near(0)
    make_columns(assign_v, cols, 0)
    make_columns(assign_v, cols, 1)
    make_turner(perm)

    def fill(b):
        first = pl.multiple_of(b * 64, 64)

        def store(a, value):
            table[pl.ds(first, 64), 128 * a : 128 * a + 128] = value.astype(BF16)

        fill_table(cols, first, 64, LON, 1.0 / math.sqrt(LON), 10, store)

    each(0, 24, fill)
    pack_one(2)
    pack_one(3)

    def lanes_of(g):
        return pl.ds(pl.multiple_of(g * 256, 256), 256)

    def y_copy(g, k):
        return to_lat(
            y.at[lat_peer(k), :, lanes_of(g)],
            x.at[lat, :, lanes_of(g)],
            y_send.at[g],
            y_recv.at[g],
            k,
        )

    def y_wait(g):
        part = pl.ds(0, NLAT - 1)
        both = to_lat(
            y.at[part, :, lanes_of(g)], x.at[part, :, lanes_of(g)], y_send.at[g], y_recv.at[g], 1
        )
        both.wait_send()
        both.wait_recv()

    def relay(h):
        near(h, 0).wait_recv()
        far(2 * h, 0).start()
        near(h, 1).wait_recv()
        far(2 * h + 1, 1).start()

    def transform(g):
        field_copy(g).wait()
        dft_group(g, table, folded_rows, perm, fields, y, lanes_of(g))
        x[lat, :, lanes_of(g)] = y[lat, :, lanes_of(g)]

    def send_group(g):
        each(1, NLAT, lambda k: y_copy(g, k).start())

    def group(g):
        transform(g)
        start_near(g + 1)
        pack_one(2 * g + 4)
        pack_one(2 * g + 5)
        send_group(g)

        @pl.when(g > 0)
        def _():
            relay(g - 1)

    each(0, 3, group)
    transform(3)
    send_group(3)
    for k in range(1, NFLD):
        extra_copy(k).start()

    levels[...] = jnp.zeros_like(levels)
    turned[...] = jnp.zeros_like(turned)
    make_pickers(pickers)
    make_columns(assign_v, cols, 2)

    def fill_inverse(b):
        first = pl.multiple_of(b * 64, 64)
        for out, size, tiles in ((t1, 1280, 10), (t2, 640, 5), (t3, 320, 3)):

            def store(a, value, out=out):
                out[pl.ds(first, 64), 128 * a : 128 * a + 128] = value.astype(BF16)

            fill_table(cols, 1536 + first, 64, size, 1.0 / math.sqrt(size), tiles, store)

    each(0, 12, fill_inverse)
    for copy in tables:
        copy.start()

    def take_group(g):
        y_wait(g)
        fold_fields(2 * g, x, folded, wide)
        fold_fields(2 * g + 1, x, folded, wide)

        @pl.when(g == 0)
        def _():
            relay(2)

        @pl.when(g == 2)
        def _():
            relay(3)
            start_last()

    each(0, 4, take_group)
    for copy in loads:
        copy.wait()
    for k in range(1, NFLD):
        extra_copy(k).wait()

    parts = ((early, early_in), (late, late_in))

    def block_copy(part, k):
        return to_lat(
            parts[part][0].at[lat_peer(k)],
            parts[part][1].at[lat],
            block_send.at[part],
            block_recv.at[part],
            k,
        )

    def pair(q):
        way = lax.rem(q, 2)
        far(q, way).wait_recv()
        p = assign_s[PAIR * lat + q]
        legendre_pair(q, p, limits, wide, main, extra, synths, joined, levels)

    def send_part(part):
        turn_levels(part, levels, turned, pickers, parts[part][0])
        parts[part][1][lat] = parts[part][0][lat]
        each(1, NLAT, lambda k: block_copy(part, k).start())

    def take_part(part):
        count = pl.ds(0, NLAT - 1)
        both = to_lat(
            parts[part][0].at[count], parts[part][1].at[count], block_send.at[part],
            block_recv.at[part], 1,
        )
        both.wait_send()
        both.wait_recv()

    each(0, EARLY, pair)
    send_part(0)
    near_last(8, 0).wait_recv()
    far(8, 0).start()
    near_last(9, 1).wait_recv()
    far(9, 1).start()
    near_last(8, 1).wait_recv()
    near_last(9, 0).wait_recv()
    each(EARLY, PAIR, pair)
    send_part(1)

    def field(f):
        part = strided(joined, 0, 6, f, 2 * PAIR, FLD)
        spec[f] = part[:, 0:641].reshape(PAIR, 2, 641).astype(BF16)

    each(0, FLD, field)
    spec_copy = pltpu.make_async_copy(spec, spec_out, store_sem.at[4])
    spec_copy.start()

    first_two = main.at[:, pl.ds(0, 2 * rows)]
    to_fld(first_two, near_send, near_recv.at[0, 0], 1).wait_send()
    to_fld(main.at[:, pl.ds(0, rows)], far_send, far_recv.at[0], 1).wait_send()
    take_part(0)
    spread_early(early_in, wide)
    for k, (table_k, p) in enumerate(((t1, p1), (t2, p2), (t3, p3))):
        first, count = LEVEL_ROWS[k]
        tiles = [wide[tile, first : first + count, :] for tile in range(4)]
        lhs = jnp.concatenate(tiles, axis=1).astype(BF16)
        p[...] = jnp.dot(lhs, table_k[0:DEEP], preferred_element_type=F32)
    products = [
        pltpu.make_async_copy(a, b, store_sem.at[5 + k])
        for k, (a, b) in enumerate(((p1, p1_out), (p2, p2_out), (p3, p3_out)))
    ]
    for copy in products:
        copy.start()
    take_part(1)
    spread_late(late_in, wide)
    done = 0
    for first, count in LEVEL_ROWS:
        rows_v[done : done + count] = wide[4, first : first + count, :].astype(BF16)
        done += count
    rows_copy = pltpu.make_async_copy(rows_v, rows_out, store_sem.at[3])
    rows_copy.start()
    for copy in products:
        copy.wait()
    for copy in tables:
        copy.wait()
    spec_copy.wait()
    rows_copy.wait()


def main_step(assign, limits, fields, legendre_t, synths):
    hbm = pl.BlockSpec(memory_space=pltpu.HBM)
    vmem = pl.BlockSpec(memory_space=pltpu.VMEM)
    smem = pl.BlockSpec(memory_space=pltpu.SMEM)
    dma = pltpu.SemaphoreType.DMA
    rows = legendre_t.shape[1]
    synths = [s.reshape(PAIR, 2, m // 2, m) for s, m in zip(synths, LEVELS)]
    wides = (1280, 640, 384)
    return pl.pallas_call(
        main_kernel,
        in_specs=[smem, smem, vmem] + [hbm] * 5,
        out_specs=[hbm] * 8,
        out_shape=[
            jax.ShapeDtypeStruct((FLD, PAIR, 2, 641), BF16),
            jax.ShapeDtypeStruct((FLD * sum(SENT), 128), BF16),
            *[jax.ShapeDtypeStruct((n, w), F32) for (_, n), w in zip(LEVEL_ROWS, wides)],
            *[jax.ShapeDtypeStruct((128, w), BF16) for w in wides],
        ],
        scratch_shapes=[
            pltpu.VMEM((PAIR, rows, 641), BF16),
            pltpu.VMEM((PAIR, NFLD * rows, 640), BF16),
            pltpu.VMEM((NFLD * rows, 128), BF16),
            pltpu.VMEM((1536, LON // 2), BF16),
            pltpu.VMEM((FLD, ROWS, LON), BF16),
            pltpu.VMEM((256, LON // 2), BF16),
            pltpu.VMEM((NLAT, 40, 1024), BF16),
            pltpu.VMEM((NLAT, 40, 1024), BF16),
            pltpu.VMEM((2, NLAT // 2, 40, 128), F32),
            pltpu.VMEM((10, 40 * FLD, 128), F32),
            pltpu.VMEM((6, 48 * PAIR, 128), F32),
            pltpu.VMEM((12, 48 * PAIR, 128), F32),
            pltpu.VMEM((512, 768), F32),
            pltpu.VMEM((FLD, PAIR, 2, 641), BF16),
            pltpu.VMEM((NLAT, 40, 384), BF16),
            pltpu.VMEM((NLAT, 40, 128), BF16),
            pltpu.VMEM((NLAT, 40, 384), BF16),
            pltpu.VMEM((NLAT, 40, 128), BF16),
            pltpu.VMEM((FLD * sum(SENT), 128), BF16),
            pltpu.VMEM((2, 640, 768), BF16),
            pltpu.VMEM((2304, 8), F32),
            pltpu.VMEM((256, 256), BF16),
            *[pltpu.VMEM(s.shape, BF16) for s in synths],
            *[pltpu.VMEM((768, w), BF16) for w in wides],
            *[pltpu.VMEM((n, w), F32) for (_, n), w in zip(LEVEL_ROWS, wides)],
            dma((PAIR,)), dma((4,)), dma((3,)), dma((8,)),
            dma((4,)), dma((4,)), dma, dma((2, 6)), dma, dma((PAIR,)),
            dma((NFLD - 1,)), dma((NFLD - 1,)), dma((2,)), dma((2,)),
        ],
        compiler_params=pltpu.CompilerParams(
            collective_id=0, has_side_effects=True, vmem_limit_bytes=64 * 1000 * 1000
        ),
    )(assign, limits, assign, fields, legendre_t, *synths)


CHUNKS = ((0, 0, 6), (0, 6, 6), (0, 12, 8), (1, 0, 10), (2, 0, 5))


def inverse_kernel(
    rows_in, spec_in, p1_in, p2_in, p3_in, t1_in, t2_in, t3_in,
    spec_out, o1_out, o2_out, o3_out,
    rows, spec, p1, p2, p3, t1, t2, t3, o1, o2, o3, in_sem, part_sem, out_sem,
):
    sums, outs = (p1, p2, p3), (o1, o2, o3)
    sources, results, tables = (p1_in, p2_in, p3_in), (o1_out, o2_out, o3_out), (t1, t2, t3)
    small = [
        pltpu.make_async_copy(a, b, in_sem.at[k])
        for k, (a, b) in enumerate(
            ((rows_in, rows), (t1_in, t1), (t2_in, t2), (t3_in, t3), (spec_in, spec))
        )
    ]
    loads, stores = [], []
    for k, (level, first, count) in enumerate(CHUNKS):
        part = pl.ds(FLD * first, FLD * count)
        loads.append(
            pltpu.make_async_copy(
                sources[level].at[part], sums[level].at[part], part_sem.at[k]
            )
        )
        part = pl.ds(first, count)
        stores.append(
            pltpu.make_async_copy(outs[level].at[part], results[level].at[part], out_sem.at[k])
        )
    for copy in small[0:2] + loads[0:3] + small[2:4] + loads[3:5] + small[4:5]:
        copy.start()
    small[0].wait()
    spec_store = pltpu.make_async_copy(spec, spec_out, out_sem.at[len(CHUNKS)])
    begin = (0, 20, 30)
    for k, (level, first, count) in enumerate(CHUNKS):
        if first == 0:
            small[1 + level].wait()
        loads[k].wait()
        start = FLD * (begin[level] + first)
        lhs = rows[start : start + FLD * count]
        z = jnp.dot(lhs, tables[level][...], preferred_element_type=F32)
        z = z + sums[level][FLD * first : FLD * (first + count)]
        size = outs[level].shape[2]
        outs[level][first : first + count] = z[:, 0:size].reshape(count, FLD, size)
        stores[k].start()
    small[4].wait()
    spec_store.start()
    for copy in stores:
        copy.wait()
    spec_store.wait()


def inverse_step(rows, spectrum, products, tables):
    shapes = [(n, FLD, 4 * m) for n, m in zip(SENT, LEVELS)]
    hbm = pl.BlockSpec(memory_space=pltpu.HBM)
    dma = pltpu.SemaphoreType.DMA
    inputs = (rows, spectrum, *products, *tables)
    return pl.pallas_call(
        inverse_kernel,
        in_specs=[hbm] * 8,
        out_specs=[hbm] * 4,
        out_shape=[jax.ShapeDtypeStruct(spectrum.shape, spectrum.dtype)]
        + [jax.ShapeDtypeStruct(s, F32) for s in shapes],
        scratch_shapes=[pltpu.VMEM(a.shape, a.dtype) for a in inputs]
        + [pltpu.VMEM(s, F32) for s in shapes]
        + [dma((5,)), dma((len(CHUNKS),)), dma((len(CHUNKS) + 1,))],
    )(*inputs)


def on_device(grid_fields, assign, limits, legendre, synth_one, synth_two, synth_three):
    spectrum, rows, *rest = main_step(
        assign,
        limits,
        grid_fields,
        jnp.transpose(legendre, (0, 2, 1)),
        (synth_one, synth_two, synth_three),
    )
    spectrum, *grids = inverse_step(rows, spectrum, rest[0:3], rest[3:6])
    return (
        jnp.transpose(spectrum, (0, 2, 1, 3)),
        *[jnp.transpose(g, (1, 0, 2)) for g in grids],
    )


def solution(mesh):
    return jax.shard_map(
        on_device,
        mesh=mesh,
        in_specs=(
            P("fld", "lat", None),
            P(),
            P(),
            P("lat", None, "fld"),
            P("lat", None, None),
            P("lat", None, None),
            P("lat", None, None),
        ),
        out_specs=(
            P("fld", None, "lat", None),
            P("fld", "lat", None),
            P("fld", "lat", None),
            P("fld", "lat", None),
        ),
        check_vma=False,
    )
```

time: 127 us -> 95.9 us (0.76); the launches traced: 125 us -> 95.8 us
  Pallas kernels: 112 us -> 95.1 us
  other arithmetic: 6.21 us -> 0 us
  local copies, waits for them, and re-layouts: 5.79 us -> 0 us
    pallas_call x2, Pallas kernels: 112 us -> 95.1 us  [the longest x1 91.4 us: main_step(): pl.pallas_call(main_kernel, in_specs=[smem, smem, vmem] + [hbm] * 5, out_...]
    le x1 -> x0, other arithmetic: 2.03 us -> none  [mask_rows(): keep = [p + 2 * k <= limits[level], p + 1 + 2 * k <= limits[level]]]
    pad x2 -> x0, local copies, waits for them, and re-layouts: 1.69 us -> none  [columns(): return jnp.pad(jnp.stack(parts, axis=-1), ((0, 0), (0, 5)))]
    slice x1 -> x0, local copies, waits for them, and re-layouts: 1.35 us -> none  [mask_rows(): keep = [p + 2 * k <= limits[level], p + 1 + 2 * k <= limits[level]]]
where the time goes in v1:
time: 95.9 us; the launch traced here: 95.8 us
  Pallas kernels  95.1 us (99%)
    pallas_call x1, Pallas kernels, main_step(): pl.pallas_call(main_kernel, in_specs=[smem, smem, vmem] + [hbm] * 5, out_...  91.4 us
    pallas_call x1, Pallas kernels, inverse_step(): pl.pallas_call(inverse_kernel, in_specs=[hbm] * 8, out_specs=[hbm] * 4, o...  3.76 us

profile of v1, /device:TPU:1, one launch (start us, length us, event | category | flops | bytes accessed | tf_op | source)
XLA Modules:
  0.0 95.8 jit_solution(18096334344796622500)
XLA Ops:
  0.6 91.4 %shard_map.102 = (bf16[24,10,2,641]{3,2,1,0:T(2,128)(2,1)}, bf16[840,128]{1,0:T(8,128)(2,1)}, f32[480,1280]{1,0:T(8,128)}, f32[240,640]{1,0:T(8,128)}, f32[120,3...) custom-call(s32[320]{0:T(512)} %assign_v.1, s32[3]{0:T(128)} %limits.1, ...), custom_call_target="tpu_custom_call" | custom-call | tf_op jit(solution)/shard_map/pallas_call | solution.py:646
  92.0 3.8 %shard_map.103 = (bf16[24,10,2,641]{3,2,1,0:T(2,128)(2,1)}, f32[20,24,1280]{2,1,0:T(8,128)}, f32[10,24,640]{2,1,0:T(8,128)}, f32[5,24,320]{2,1,0:T(8,128)}) custom-call(bf16[840,128]{1,0:T(8,128)(2,1)} %get-tuple-element.16.rows_in, bf16[24,10,2,641]{3,2,1,0:T(2,128)(2,1)} %get-tuple-element.17.spec_in, f32[480,1280]{1,0:T(8,128)} %get-tuple-element.18.p1_in, ...), custom_call_target="tpu_custom_call" | custom-call | tf_op jit(solution)/shard_map/pallas_call | solution.py:748

commit v2 on v1

--- a/solution.py
+++ b/solution.py
@@ -166,8 +166,10 @@
         late = r >= 512.0
         s = jnp.where(late, r - 512.0, r)
         valid = r < 640.0
-        l = jnp.where(late, jnp.floor((s + 0.5) * 0.25), jnp.floor((s + 0.5) * (1.0 / 16)))
-        i = s - jnp.where(late, 4.0, 16.0) * l
+        high_part = jnp.floor((s + 0.5) * jnp.where(late, 1.0 / 32, 1.0 / 16))
+        low_part = s - jnp.where(late, 32.0, 16.0) * high_part
+        l = jnp.where(late, low_part, high_part)
+        i = jnp.where(late, high_part, low_part)
         q = jnp.floor(i * 0.5) + jnp.where(late, 8.0, 0.0)
     slot = jnp.where(valid, 10.0 * l + q, -1.0)
     lane = lax.broadcasted_iota(jnp.int32, (768, value.shape[1]), 1).astype(F32)
@@ -180,7 +182,7 @@
     rows = slice(768 * part, 768 * part + 768)
     cols[rows, 0:1] = wave
     cols[rows, 1:2] = amp
-    cols[rows, 2:3] = r - 2.0 * jnp.floor(r * 0.5)
+    cols[rows, 2:3] = i - 2.0 * jnp.floor(i * 0.5)
 
 
 def make_turner(perm):
@@ -315,13 +317,19 @@
 
 def turn_levels(part, levels, turned, pickers, blocks):
     half = NLAT // 2
-    count = 2 * (EARLY if part == 0 else PAIR - EARLY)
     base = 0 if part == 0 else 2 * EARLY * FLD
     size = blocks.shape[2]
     for sign in range(2):
-        for f in range(FLD):
-            value = strided(levels, 6 * sign, 6, base + f, count, FLD)
-            turned[base + count * f : base + count * f + count] = value
+        if part == 0:
+            for f in range(FLD):
+                value = strided(levels, 6 * sign, 6, f, 2 * EARLY, FLD)
+                turned[2 * EARLY * f : 2 * EARLY * (f + 1)] = value
+        else:
+            for i in range(2 * (PAIR - EARLY)):
+                first = base + FLD * i
+                tiles = [levels[6 * sign + k, first : first + FLD, :] for k in range(6)]
+                first = base + 32 * i
+                turned[first : first + FLD] = jnp.concatenate(tiles, axis=1)
         picked = lax.dot_general(
             pickers[sign],
             turned[base : base + size].astype(BF16),
@@ -366,7 +374,7 @@
     def rows(b):
         own = pl.ds(pl.multiple_of(8 * b, 8), 8)
         values = [arrived[l, own, :].astype(F32) for l in range(NLAT)]
-        for f, value in enumerate(swap_units(values, 4)[0:FLD]):
+        for f, value in enumerate(swap_units(values, 1)[0:FLD]):
             wide[4, pl.ds(8 * FLD * b + f, 8, stride=FLD), :] = value
 
     each(0, 5, rows)
@@ -406,12 +414,11 @@
         for k, (a, b) in enumerate(((t1, t1_out), (t2, t2_out), (t3, t3_out)))
     ]
     each(0, PAIR, lambda q: raw_copy(q).start())
+    all_greeted = greet()
     each(0, 4, lambda g: field_copy(g).start())
     for copy in loads:
         copy.start()
-    all_greeted = greet()
     extra[own] = jnp.zeros((rows, 128), BF16)
-    folded_rows[...] = jnp.zeros_like(folded_rows)
 
     def shard(q, k):
         s = lax.rem(fld + k, NFLD)
@@ -448,6 +455,9 @@
     pack_one(1)
     all_greeted()
     start_near(0)
+    pack_one(2)
+    pack_one(3)
+    folded_rows[...] = jnp.zeros_like(folded_rows)
     make_columns(assign_v, cols, 0)
     make_columns(assign_v, cols, 1)
     make_turner(perm)
@@ -461,8 +471,7 @@
         fill_table(cols, first, 64, LON, 1.0 / math.sqrt(LON), 10, store)
 
     each(0, 24, fill)
-    pack_one(2)
-    pack_one(3)
+    start_near(1)
 
     def lanes_of(g):
         return pl.ds(pl.multiple_of(g * 256, 256), 256)
@@ -500,10 +509,13 @@
 
     def group(g):
         transform(g)
-        start_near(g + 1)
         pack_one(2 * g + 4)
         pack_one(2 * g + 5)
         send_group(g)
+
+        @pl.when(g < 2)
+        def _():
+            start_near(g + 2)
 
         @pl.when(g > 0)
         def _():

time: 95.9 us -> 95 us (level)
  no operation moved by 1% of the time
where the time goes in v2:
time: 95 us; the launch traced here: 94.8 us
  Pallas kernels  94.2 us (99%)
    pallas_call x1, Pallas kernels, main_step(): pl.pallas_call(main_kernel, in_specs=[smem, smem, vmem] + [hbm] * 5, out_...  90.4 us
    pallas_call x1, Pallas kernels, inverse_step(): pl.pallas_call(inverse_kernel, in_specs=[hbm] * 8, out_specs=[hbm] * 4, o...  3.76 us

profile of v2, /device:TPU:1, one launch (start us, length us, event | category | flops | bytes accessed | tf_op | source)
XLA Modules:
  0.0 94.8 jit_solution(8958733924499730167)
XLA Ops:
  0.6 90.4 %shard_map.102 = (bf16[24,10,2,641]{3,2,1,0:T(2,128)(2,1)}, bf16[840,128]{1,0:T(8,128)(2,1)}, f32[480,1280]{1,0:T(8,128)}, f32[240,640]{1,0:T(8,128)}, f32[120,3...) custom-call(s32[320]{0:T(512)} %assign_v.1, s32[3]{0:T(128)} %limits.1, ...), custom_call_target="tpu_custom_call" | custom-call | tf_op jit(solution)/shard_map/pallas_call | solution.py:658
  91.1 3.8 %shard_map.103 = (bf16[24,10,2,641]{3,2,1,0:T(2,128)(2,1)}, f32[20,24,1280]{2,1,0:T(8,128)}, f32[10,24,640]{2,1,0:T(8,128)}, f32[5,24,320]{2,1,0:T(8,128)}) custom-call(bf16[840,128]{1,0:T(8,128)(2,1)} %get-tuple-element.16.rows_in, bf16[24,10,2,641]{3,2,1,0:T(2,128)(2,1)} %get-tuple-element.17.spec_in, f32[480,1280]{1,0:T(8,128)} %get-tuple-element.18.p1_in, ...), custom_call_target="tpu_custom_call" | custom-call | tf_op jit(solution)/shard_map/pallas_call | solution.py:760

commit v3 on v2

--- a/solution.py
+++ b/solution.py
@@ -386,7 +386,7 @@
 def main_kernel(
     assign_s, limits, assign_v, fields_in, legendre_in, s1_in, s2_in, s3_in,
     spec_out, rows_out, p1_out, p2_out, p3_out, t1_out, t2_out, t3_out,
-    raw, main, extra, table, fields, folded_rows, y, x, folded, wide, joined, levels, turned,
+    raw, main, extra, columns, table, fields, folded_rows, y, x, folded, wide, joined, levels, turned,
     spec, early, late, early_in, late_in, rows_v, pickers, cols, perm, s1, s2, s3, t1, t2, t3,
     p1, p2, p3,
     raw_sem, field_sem, load_sem, store_sem, y_send, y_recv, near_send, near_recv,
@@ -435,7 +435,7 @@
         return to_fld(shard(q, 3 - 2 * way), far_send, far_recv.at[q], 1 + 2 * way)
 
     def extra_copy(k):
-        return to_fld(extra.at[own], extra_send.at[k - 1], extra_recv.at[k - 1], k)
+        return to_fld(columns.at[fld], extra_send.at[k - 1], extra_recv.at[k - 1], k)
 
     def start_near(h):
         near(h, 0).start()
@@ -524,12 +524,18 @@
     each(0, 3, group)
     transform(3)
     send_group(3)
-    for k in range(1, NFLD):
-        extra_copy(k).start()
+    unit = lax.broadcasted_iota(jnp.int32, (16, 128), 0)
+    unit = jnp.where(unit == lax.broadcasted_iota(jnp.int32, (16, 128), 1), 1.0, 0.0).astype(BF16)
+    columns[fld] = jnp.zeros((16, 256), BF16)
+    columns[fld, :, 0:rows] = lax.dot_general(
+        unit, extra[own], NT, preferred_element_type=F32
+    ).astype(BF16)
 
     levels[...] = jnp.zeros_like(levels)
     turned[...] = jnp.zeros_like(turned)
     make_pickers(pickers)
+    for k in range(1, NFLD):
+        extra_copy(k).start()
     make_columns(assign_v, cols, 2)
 
     def fill_inverse(b):
@@ -564,6 +570,11 @@
         copy.wait()
     for k in range(1, NFLD):
         extra_copy(k).wait()
+    for k in range(NFLD):
+        back = lax.dot_general(
+            columns[k, :, 0:rows], unit, (((0,), (0,)), ((), ())), preferred_element_type=F32
+        )
+        extra[rows * k : rows * k + rows] = back.astype(BF16)
 
     parts = ((early, early_in), (late, late_in))
 
@@ -669,6 +680,7 @@
             pltpu.VMEM((PAIR, rows, 641), BF16),
             pltpu.VMEM((PAIR, NFLD * rows, 640), BF16),
             pltpu.VMEM((NFLD * rows, 128), BF16),
+            pltpu.VMEM((NFLD, 16, 256), BF16),
             pltpu.VMEM((1536, LON // 2), BF16),
             pltpu.VMEM((FLD, ROWS, LON), BF16),
             pltpu.VMEM((256, LON // 2), BF16),

time: 95 us -> 93.6 us (0.985)
  Pallas kernels: 94.2 us -> 92.8 us
    pallas_call x1, Pallas kernels: 90.4 us -> 89 us  [main_step(): pl.pallas_call(main_kernel, in_specs=[smem, smem, vmem] + [hbm] * 5, out_...]
where the time goes in v3:
time: 93.6 us; the launch traced here: 93.4 us
  Pallas kernels  92.8 us (99%)
    pallas_call x1, Pallas kernels, main_step(): pl.pallas_call(main_kernel, in_specs=[smem, smem, vmem] + [hbm] * 5, out_...  89 us
    pallas_call x1, Pallas kernels, inverse_step(): pl.pallas_call(inverse_kernel, in_specs=[hbm] * 8, out_specs=[hbm] * 4, o...  3.76 us

profile of v3, /device:TPU:1, one launch (start us, length us, event | category | flops | bytes accessed | tf_op | source)
XLA Modules:
  0.0 93.4 jit_solution(11305218182927108785)
XLA Ops:
  0.6 89.0 %shard_map.102 = (bf16[24,10,2,641]{3,2,1,0:T(2,128)(2,1)}, bf16[840,128]{1,0:T(8,128)(2,1)}, f32[480,1280]{1,0:T(8,128)}, f32[240,640]{1,0:T(8,128)}, f32[120,3...) custom-call(s32[320]{0:T(512)} %assign_v.1, s32[3]{0:T(128)} %limits.1, ...), custom_call_target="tpu_custom_call" | custom-call | tf_op jit(solution)/shard_map/pallas_call | solution.py:669
  89.7 3.8 %shard_map.103 = (bf16[24,10,2,641]{3,2,1,0:T(2,128)(2,1)}, f32[20,24,1280]{2,1,0:T(8,128)}, f32[10,24,640]{2,1,0:T(8,128)}, f32[5,24,320]{2,1,0:T(8,128)}) custom-call(bf16[840,128]{1,0:T(8,128)(2,1)} %get-tuple-element.16.rows_in, bf16[24,10,2,641]{3,2,1,0:T(2,128)(2,1)} %get-tuple-element.17.spec_in, f32[480,1280]{1,0:T(8,128)} %get-tuple-element.18.p1_in, ...), custom_call_target="tpu_custom_call" | custom-call | tf_op jit(solution)/shard_map/pallas_call | solution.py:772

commit v4 on v3

--- a/solution.py
+++ b/solution.py
@@ -587,9 +587,10 @@
             k,
         )
 
+    def whole(q):
+        far(q, lax.rem(q, 2)).wait_recv()
+
     def pair(q):
-        way = lax.rem(q, 2)
-        far(q, way).wait_recv()
         p = assign_s[PAIR * lat + q]
         legendre_pair(q, p, limits, wide, main, extra, synths, joined, levels)
 
@@ -607,7 +608,11 @@
         both.wait_send()
         both.wait_recv()
 
-    each(0, EARLY, pair)
+    def early_pair(q):
+        whole(q)
+        pair(q)
+
+    each(0, EARLY, early_pair)
     send_part(0)
     near_last(8, 0).wait_recv()
     far(8, 0).start()
@@ -615,7 +620,10 @@
     far(9, 1).start()
     near_last(8, 1).wait_recv()
     near_last(9, 0).wait_recv()
-    each(EARLY, PAIR, pair)
+    for q in range(EARLY, PAIR):
+        whole(q)
+    for q in range(EARLY, PAIR):
+        pair(q)
     send_part(1)
 
     def field(f):

time: 93.6 us -> 93.4 us (level)
  no operation moved by 1% of the time
where the time goes in v4:
time: 93.4 us; the launch traced here: 93.2 us
  Pallas kernels  92.6 us (99%)
    pallas_call x1, Pallas kernels, main_step(): pl.pallas_call(main_kernel, in_specs=[smem, smem, vmem] + [hbm] * 5, out_...  88.8 us
    pallas_call x1, Pallas kernels, inverse_step(): pl.pallas_call(inverse_kernel, in_specs=[hbm] * 8, out_specs=[hbm] * 4, o...  3.76 us

profile of v4, /device:TPU:1, one launch (start us, length us, event | category | flops | bytes accessed | tf_op | source)
XLA Modules:
  0.0 93.2 jit_solution(18314990378845471389)
XLA Ops:
  0.6 88.8 %shard_map.102 = (bf16[24,10,2,641]{3,2,1,0:T(2,128)(2,1)}, bf16[840,128]{1,0:T(8,128)(2,1)}, f32[480,1280]{1,0:T(8,128)}, f32[240,640]{1,0:T(8,128)}, f32[120,3...) custom-call(s32[320]{0:T(512)} %assign_v.1, s32[3]{0:T(128)} %limits.1, ...), custom_call_target="tpu_custom_call" | custom-call | tf_op jit(solution)/shard_map/pallas_call | solution.py:677
  89.5 3.8 %shard_map.103 = (bf16[24,10,2,641]{3,2,1,0:T(2,128)(2,1)}, f32[20,24,1280]{2,1,0:T(8,128)}, f32[10,24,640]{2,1,0:T(8,128)}, f32[5,24,320]{2,1,0:T(8,128)}) custom-call(bf16[840,128]{1,0:T(8,128)(2,1)} %get-tuple-element.16.rows_in, bf16[24,10,2,641]{3,2,1,0:T(2,128)(2,1)} %get-tuple-element.17.spec_in, f32[480,1280]{1,0:T(8,128)} %get-tuple-element.18.p1_in, ...), custom_call_target="tpu_custom_call" | custom-call | tf_op jit(solution)/shard_map/pallas_call | solution.py:780
